TPU v7x, 128 devices: a whole 4x4x4 slice. The times are simulated.
128 devices in a mesh: ep: 32 (over y, x, core), tp: 4 (over z).
Axes of the slice: x: 4, y: 4, z: 4, core: 2. Of those that a mesh axis runs over, the one named last changes fastest.
Arguments:
- tokens: bfloat16 [8192, 7168], P('ep', 'tp'), may hold values from -78 to 78
- norm_gain: bfloat16 [7168], P('tp'), may hold values from 0.5 to 1.5
- expert_ids: int32 [8192, 8], P('ep'), may hold values from 0 to 255, all different within a row
- gate_prob: bfloat16 [8192, 8], P('ep'), may hold values from 0.049804688 to 1
- w_gate: bfloat16 [32, 7168, 2048], P('ep', None, 'tp'), may hold values from -0.0625 to 0.0625
- w_up: bfloat16 [32, 7168, 2048], P('ep', None, 'tp'), may hold values from -0.0625 to 0.0625
- w_down: bfloat16 [32, 2048, 7168], P('ep', 'tp'), may hold values from -0.125 to 0.125
Outputs:
- combined: bfloat16 [8192, 7168], P('ep', 'tp')
Inputs may be any that keep to these rules, and one draw needn't show every extreme that they name: `expert_ids`: each row names 8 different experts.
All inputs are finite; a program needn't handle non-finite values.
Results may differ from a plain program's by a relative error of at most 0.01.
Values may be sent and summed in bfloat16 or wider, within the bound.
No kernel may reach another device: no remote copies, remote signals or barrier semaphores. Data moves between devices by JAX's collectives and lax.ppermute only.
A program may use at most 128 MiB of HBM per device.

v0:
```python
import jax
import jax.numpy as jnp
from jax import lax
from jax.sharding import PartitionSpec as P

D = 7168
TOP = 8
EXP_DEV = 8
epsilon = 1e-06


def from_everyone(value, axis):
    length = lax.axis_size(axis)
    return lax.all_to_all(
        jnp.broadcast_to(value[None], (length, *value.shape)), axis, 0, 0, tiled=True
    )


def over_copies(value, axis):
    everything = from_everyone(value, axis)
    return jnp.sum(everything, axis=0)


def exchange_in_groups(value, axis, split_dim, concat_dim, work, item_dim, out_dim):
    items = jax.tree.leaves(value)[0].shape[item_dim]
    count = 2 if items % 2 == 0 else 1
    done = []
    for k in range(count):
        group = jax.tree.map(
            lambda a: lax.slice_in_dim(
                a, k * (items // count), (k + 1) * (items // count), axis=item_dim
            ),
            value,
        )
        done.append(
            work(
                lax.all_to_all(
                    group, axis, split_axis=split_dim, concat_axis=concat_dim, tiled=True
                )
            )
        )
    return jax.tree.map(lambda *parts: jnp.concatenate(parts, axis=out_dim), *done)


def place_picks(expert_ids, gate_prob, window, capacity):
    is_live = expert_ids < window
    matches = (expert_ids[:, :, None] == jnp.arange(window, dtype=jnp.int32)).astype(jnp.int32)
    counts = jnp.sum(matches, axis=1)
    before = jnp.cumsum(counts, axis=0) - counts
    slot_index = jnp.sum(matches * before[:, None, :], axis=2)
    is_kept = is_live & (slot_index < capacity)
    target = jnp.where(is_kept, expert_ids * capacity + slot_index, -1)
    hit_table = target[:, :, None] == jnp.arange(window * capacity, dtype=jnp.int32)
    dispatch_mat = jnp.any(hit_table, axis=1).astype(jnp.bfloat16)
    weight_mat = jnp.sum(
        jnp.where(hit_table, gate_prob.astype(jnp.float32)[:, :, None], 0.0), axis=1
    ).astype(jnp.bfloat16)
    return (dispatch_mat, weight_mat)


def run_expert(received, w_gate, w_up, w_down):
    senders, item_count, row_width = received.shape
    flat_rows = received.reshape(senders * item_count, row_width)
    gate_act = jnp.dot(flat_rows, w_gate[0], preferred_element_type=jnp.float32)
    up_act = jnp.dot(flat_rows, w_up[0], preferred_element_type=jnp.float32)
    hidden = (jax.nn.silu(gate_act) * up_act).astype(jnp.bfloat16)
    down_term = jnp.einsum("rf,fc->rc", hidden, w_down[0], preferred_element_type=jnp.float32)
    summed = lax.psum_scatter(down_term.astype(jnp.bfloat16), "tp", scatter_dimension=1, tiled=True)
    shares = summed.reshape(senders, item_count, -1)
    return lax.all_to_all(shares, "ep", split_axis=0, concat_axis=0, tiled=True)


def local(tokens, norm_gain, expert_ids, gate_prob, w_gate, w_up, w_down):
    window = lax.axis_size("ep")
    tok_rows = tokens.shape[0]
    capacity = max(2, 2 * tok_rows * TOP // (EXP_DEV * window))
    dispatch_mat, weight_mat = place_picks(expert_ids, gate_prob, window, capacity)
    values = tokens.astype(jnp.float32)
    square_part = jnp.sum(values * values, axis=1)
    square_total = over_copies(square_part, "tp")
    inverse_rms = lax.rsqrt(square_total / D + epsilon)
    normed = (values * inverse_rms[:, None] * norm_gain.astype(jnp.float32)).astype(jnp.bfloat16)
    outgoing = jnp.einsum("tp,td->pd", dispatch_mat, normed, preferred_element_type=jnp.float32)
    outgoing = outgoing.astype(jnp.bfloat16).reshape(window, capacity, -1)

    def handle(received):
        gathered = lax.all_gather(received, "tp", axis=2, tiled=True)
        return run_expert(gathered, w_gate, w_up, w_down)

    returned = exchange_in_groups(outgoing, "ep", 0, 0, handle, 1, 1)
    flat_back = returned.reshape(-1, returned.shape[2])
    combined = jnp.einsum("tp,pd->td", weight_mat, flat_back, preferred_element_type=jnp.float32)
    return combined.astype(jnp.bfloat16)


def solution(mesh):
    placed = (
        P("ep", "tp"),
        P("tp"),
        P("ep", None),
        P("ep", None),
        P("ep", None, "tp"),
        P("ep", None, "tp"),
        P("ep", "tp", None),
    )
    return jax.shard_map(
        local, mesh=mesh, in_specs=placed, out_specs=P("ep", "tp"), check_vma=False
    )
```

profile of v0, /device:TPU:1, one launch (start us, length us, event | category | flops | bytes accessed | tf_op | source)
XLA Modules:
  0.0 255.4 jit_solution(9727998538408173753)
XLA Ops:
  6.5 1.4 fusion.15
  8.0 0.6 broadcast_in_dim.21
  8.6 5.8 %all-to-all-start = ((f32[4,1,256]{2,1,0:T(1,128)}), f32[4,1,256]{2,1,0:T(1,128)S(1)}, u32[]{:S(2)}, u32[]{:S(2)}) async-start(f32[4,1,256]{2,1,0:T(1,128)} %broadcast_in_dim.21), calls=%async_computation | async-start | bytes 8192 | tf_op jit(solution)/shard_map/all_to_all | solution.py:14
  14.4 0.0 all-gather.3.cloned.1.call-start
  14.4 0.7 convert_reduce_fusion
  15.2 0.6 reduce-window.6
  15.8 0.2 slice_reduce_fusion
  16.0 0.1 fusion.52
  16.1 0.8 select_reduce_fusion.1
  16.8 0.7 add_select_fusion
  17.5 0.1 copy.23
  17.7 1.7 fusion.10
  19.4 0.7 convert_element_type.41
  20.1 0.0 all-to-all-done
  20.1 2.0 convolution_convert_fusion.2
  22.1 0.1 fusion.55
  22.3 23.6 %all_to_all.26 = bf16[32,8,1792]{2,1,0:T(8,128)(2,1)} all-to-all(bf16[32,8,1792]{2,1,0:T(8,128)(2,1)S(1)} %get-tuple-element.5), channel_id=1, replica_groups=mesh['ep'=32,'tp'=4] {'ep'}, dimensions={0} | all-to-all | bytes 1835008 | tf_op jit(solution)/shard_map/all_to_all | solution.py:37
  45.9 0.0 all-gather.3.cloned.1.call-update
  45.9 0.0 all-gather.5.cloned.1.call-start
  45.9 19.5 %all_to_all.27 = bf16[32,8,1792]{2,1,0:T(8,128)(2,1)} all-to-all(bf16[32,8,1792]{2,1,0:T(8,128)(2,1)S(1)} %get-tuple-element.6), channel_id=1, replica_groups=mesh['ep'=32,'tp'=4] {'ep'}, dimensions={0} | all-to-all | bytes 1835008 | tf_op jit(solution)/shard_map/all_to_all | solution.py:37
  65.4 0.0 all-gather.5.cloned.1.call-update
  65.5 0.0 reduce-scatter.3.cloned.1.call-start
  65.5 22.4 %all-gather.3.cloned.1.call-done = bf16[32,8,7168]{2,1,0:T(8,128)(2,1)} async-done(((bf16[32,8,1792]{2,1,0:T(8,128)(2,1)}), bf16[32,8,7168]{2,1,0:T(8,128)(2,1)}) %all-gather.3.cloned.1.call-update) | async-done | bytes 3670032 | tf_op jit(solution)/shard_map/all_gather | solution.py:87
  87.9 6.2 %fusion.8 = f32[256,512]{1,0:T(8,128)S(1)} fusion(bf16[1,7168,512]{2,1,0:T(8,128)(2,1)} %param.11, bf16[32,8,7168]{2,1,0:T(8,128)(2,1)} %all-gather.3.cloned.1.call-done), kind=kOutput, calls=%fused_computation.10 | convolution fusion | flops 1879048192 | bytes 11534336 | tf_op jit(solution)/shard_map/dot_general | solution.py:64
  94.1 12.6 %convolution_convert_fusion.1 = bf16[256,7168]{1,0:T(8,128)(2,1)} fusion(bf16[1,512,7168]{2,1,0:T(8,128)(2,1)} %param.13, bf16[1,7168,512]{2,1,0:T(8,128)(2,1)} %param.12, bf16[32,8,7168]{2,1,0:T(8,128)(2,1)} %all-gather.3.cloned.1.call-done, f32[256,512]{1,0:T(8,128)S(1)} %fusion.8), kind=kOutput, calls=%fused_computation.1 | convolution fusion | flops 3760717824 | bytes 22544384 | tf_op jit(solution)/shard_map/rf,fc->rc/dot_general | solution.py:67
  106.8 0.0 reduce-scatter.3.cloned.1.call-update
  106.8 0.2 reduce-scatter.5.cloned.1.call-start
  107.0 26.7 %all-gather.5.cloned.1.call-done = bf16[32,8,7168]{2,1,0:T(8,128)(2,1)} async-done(((bf16[32,8,1792]{2,1,0:T(8,128)(2,1)}), bf16[32,8,7168]{2,1,0:T(8,128)(2,1)}) %all-gather.5.cloned.1.call-update) | async-done | bytes 3670032 | tf_op jit(solution)/shard_map/all_gather | solution.py:87
  133.8 6.2 %fusion.6 = f32[256,512]{1,0:T(8,128)S(1)} fusion(bf16[1,7168,512]{2,1,0:T(8,128)(2,1)} %param.11, bf16[32,8,7168]{2,1,0:T(8,128)(2,1)} %all-gather.5.cloned.1.call-done), kind=kOutput, calls=%fused_computation.8 | convolution fusion | flops 1879048192 | bytes 11534336 | tf_op jit(solution)/shard_map/dot_general | solution.py:64
  140.0 12.8 %convolution_convert_fusion = bf16[256,7168]{1,0:T(8,128)(2,1)} fusion(bf16[1,512,7168]{2,1,0:T(8,128)(2,1)} %param.13, bf16[1,7168,512]{2,1,0:T(8,128)(2,1)} %param.12, bf16[32,8,7168]{2,1,0:T(8,128)(2,1)} %all-gather.5.cloned.1.call-done, f32[256,512]{1,0:T(8,128)S(1)} %fusion.6), kind=kOutput, calls=%fused_computation | convolution fusion | flops 3760717824 | bytes 22544384 | tf_op jit(solution)/shard_map/rf,fc->rc/dot_general | solution.py:67
  152.8 0.0 copy-start
  152.8 0.0 reduce-scatter.5.cloned.1.call-update
  152.9 26.3 %reduce-scatter.3.cloned.1.call-done = bf16[256,1792]{1,0:T(8,128)(2,1)} async-done(((bf16[256,7168]{1,0:T(8,128)(2,1)}), bf16[256,1792]{1,0:T(8,128)(2,1)}) %reduce-scatter.3.cloned.1.call-update) | async-done | bytes 917520 | tf_op jit(solution)/shard_map/reduce_scatter | solution.py:68
  179.2 7.6 %all-to-all-start.2 = ((bf16[32,8,1792]{2,1,0:T(8,128)(2,1)}), bf16[32,8,1792]{2,1,0:T(8,128)(2,1)S(1)}, u32[]{:S(2)}, u32[]{:S(2)}) async-start(bf16[32,8,1792]{2,1,0:T(8,128)(2,1)} %bitcast.75), calls=%async_computation.3 | async-start | bytes 1835008 | tf_op jit(solution)/shard_map/all_to_all | solution.py:70
  186.8 37.1 %reduce-scatter.5.cloned.1.call-done = bf16[256,1792]{1,0:T(8,128)(2,1)} async-done(((bf16[256,7168]{1,0:T(8,128)(2,1)}), bf16[256,1792]{1,0:T(8,128)(2,1)}) %reduce-scatter.5.cloned.1.call-update) | async-done | bytes 917520 | tf_op jit(solution)/shard_map/reduce_scatter | solution.py:68
  223.9 0.0 all-to-all-done.2
  223.9 7.6 %all-to-all-start.4 = ((bf16[32,8,1792]{2,1,0:T(8,128)(2,1)}), bf16[32,8,1792]{2,1,0:T(8,128)(2,1)S(1)}, u32[]{:S(2)}, u32[]{:S(2)}) async-start(bf16[32,8,1792]{2,1,0:T(8,128)(2,1)} %bitcast.76), calls=%async_computation.6 | async-start | bytes 1835008 | tf_op jit(solution)/shard_map/all_to_all | solution.py:70
  231.5 0.0 copy-done
  231.5 0.1 copy.24
  231.6 1.7 select_reduce_fusion
  233.3 13.8 %all-to-all-done.4 = bf16[32,8,1792]{2,1,0:T(8,128)(2,1)S(1)} async-done(((bf16[32,8,1792]{2,1,0:T(8,128)(2,1)}), bf16[32,8,1792]{2,1,0:T(8,128)(2,1)S(1)}, u32[]{:S(2)}, u32[]{:S(2)}) %all-to-all-start.4) | async-done | bytes 917536 | tf_op jit(solution)/shard_map/all_to_all | solution.py:70
  247.1 0.1 pad_maximum_fusion
  247.3 1.6 convolution_convert_fusion.3
  (5 shorter events, 0.1 us)
Async XLA Ops:
  8.6 11.5 %all-to-all-start = ((f32[4,1,256]{2,1,0:T(1,128)}), f32[4,1,256]{2,1,0:T(1,128)S(1)}, u32[]{:S(2)}, u32[]{:S(2)}) async-start(f32[4,1,256]{2,1,0:T(1,128)} %broadcast_in_dim.21), calls=%async_computation | async-start | bytes 8192 | tf_op jit(solution)/shard_map/all_to_all | solution.py:14
  14.4 73.5 %all-gather.3.cloned.1.call-start = ((), (), s32[]{:S(2)}) async-start(), calls=%async_computation.7 | async-start | bytes 4587520 | tf_op jit(solution)/shard_map/all_gather | solution.py:87
  45.9 87.9 %all-gather.5.cloned.1.call-start = ((), (), s32[]{:S(2)}) async-start(), calls=%async_computation.9 | async-start | bytes 4587520 | tf_op jit(solution)/shard_map/all_gather | solution.py:87
  65.5 113.8 %reduce-scatter.3.cloned.1.call-start = ((), (), s32[]{:S(2)}) async-start(), calls=%async_computation.8 | async-start | bytes 4587520 | tf_op jit(solution)/shard_map/reduce_scatter | solution.py:68
  106.8 117.1 %reduce-scatter.5.cloned.1.call-start = ((), (), s32[]{:S(2)}) async-start(), calls=%async_computation.10 | async-start | bytes 4587520 | tf_op jit(solution)/shard_map/reduce_scatter | solution.py:68
  152.8 78.6 %copy-start = (bf16[256,8]{0,1:T(8,128)(2,1)S(1)}, bf16[256,8]{0,1:T(8,128)(2,1)}, u32[]{:S(2)}) copy-start(bf16[256,8]{0,1:T(8,128)(2,1)} %param.10) | copy-start | bytes 12292
  179.2 44.7 %all-to-all-start.2 = ((bf16[32,8,1792]{2,1,0:T(8,128)(2,1)}), bf16[32,8,1792]{2,1,0:T(8,128)(2,1)S(1)}, u32[]{:S(2)}, u32[]{:S(2)}) async-start(bf16[32,8,1792]{2,1,0:T(8,128)(2,1)} %bitcast.75), calls=%async_computation.3 | async-start | bytes 1835008 | tf_op jit(solution)/shard_map/all_to_all | solution.py:70
  223.9 23.2 %all-to-all-start.4 = ((bf16[32,8,1792]{2,1,0:T(8,128)(2,1)}), bf16[32,8,1792]{2,1,0:T(8,128)(2,1)S(1)}, u32[]{:S(2)}, u32[]{:S(2)}) async-start(bf16[32,8,1792]{2,1,0:T(8,128)(2,1)} %bitcast.76), calls=%async_computation.6 | async-start | bytes 1835008 | tf_op jit(solution)/shard_map/all_to_all | solution.py:70
Sparse Core Ops, SparseCore 0:
  46.0 41.8 all-gather.2
  89.6 44.1 all-gather.4
  136.2 42.9 reduce-scatter.2
  181.5 42.3 reduce-scatter.4
where the time goes:
time: 256 us; the launch traced here: 255 us
  waiting for transfers between devices  126 us (49%)
  blocking collectives  43.1 us (17%)
  matrix products  41.6 us (16%)
  starting transfers between devices  21.3 us (8%)
  between operations  13.2 us (5%)
  other arithmetic  8.58 us (3%)
    reduce_scatter x2, waiting for transfers between devices, run_expert(): lax.psum_scatter(down_term.astype(jnp.bfloat16), 'tp', scatter_dimension=...  63.4 us
    all_gather x2, waiting for transfers between devices, handle(): gathered = lax.all_gather(received, 'tp', axis=2, tiled=True)  49.1 us
    all_to_all x2, blocking collectives, exchange_in_groups(): lax.all_to_all(group, axis, split_axis=split_dim, concat_axis=concat_dim,...  43.1 us
    dot_general x2, matrix products, run_expert(): jnp.einsum('rf,fc->rc', hidden, w_down[0], preferred_element_type=jnp.flo...  25.5 us
    all_to_all x2, starting transfers between devices, run_expert(): return lax.all_to_all(shares, 'ep', split_axis=0, concat_axis=0, tiled=True)  15.2 us
    all_to_all x2, waiting for transfers between devices, run_expert(): return lax.all_to_all(shares, 'ep', split_axis=0, concat_axis=0, tiled=True)  13.8 us
    dot_general x2, matrix products, run_expert(): gate_act = jnp.dot(flat_rows, w_gate[0], preferred_element_type=jnp.float32)  12.5 us
    all_to_all x1, starting transfers between devices, from_everyone(): lax.all_to_all(jnp.broadcast_to(value[None], (length, *value.shape)), axi...  5.84 us
  transfers between devices with their start and end apart: 7, of which 5 were waited for; matrix products, arithmetic and copies ran while one was open for 18% of the time, Pallas kernels for 0%

commit v1 on v0

--- a/solution.py
+++ b/solution.py
@@ -84,7 +84,9 @@
     outgoing = outgoing.astype(jnp.bfloat16).reshape(window, capacity, -1)
 
     def handle(received):
-        gathered = lax.all_gather(received, "tp", axis=2, tiled=True)
+        gathered = jnp.concatenate(
+            lax.all_to_all(jnp.stack([received] * lax.axis_size("tp")), "tp", 0, 0), axis=2
+        )
         return run_expert(gathered, w_gate, w_up, w_down)
 
     returned = exchange_in_groups(outgoing, "ep", 0, 0, handle, 1, 1)

time: 256 us -> 285 us (1.11)
  blocking collectives: 43.1 us -> 148 us
  waiting for transfers between devices: 126 us -> 48.4 us
  local copies, waits for them, and re-layouts: 1.14 us -> 12.3 us
  matrix products: 41.6 us -> 32 us
    all_to_all x0 -> x2, blocking collectives: none -> 104 us  [handle(): lax.all_to_all(jnp.stack([received] * lax.axis_size('tp')), 'tp', 0, 0)]
    all_gather x2 -> x0, waiting for transfers between devices: 49.1 us -> none  [handle(): gathered = lax.all_gather(received, 'tp', axis=2, tiled=True)]
    reduce_scatter x2, waiting for transfers between devices: 63.4 us -> 34.5 us  [run_expert(): lax.psum_scatter(down_term.astype(jnp.bfloat16), 'tp', scatter_dimension=...]
    dot_general x2, matrix products: 12.5 us -> 4.28 us  [run_expert(): gate_act = jnp.dot(flat_rows, w_gate[0], preferred_element_type=jnp.float32)]
    reshape x1 -> x3, local copies, waits for them, and re-layouts: 0.01 us -> 5.67 us  [the longest x2 5.67 us: handle(): jnp.concatenate(lax.all_to_all(jnp.stack([received] * lax.axis_size('tp')...]
    unnamed x2 -> x16, local copies, waits for them, and re-layouts: 0.01 us -> 5.07 us
  transfers between devices with their start and end apart: 7 -> 5, of which waited for: 5 -> 2; matrix products, arithmetic and copies ran while one was open for 18% -> 9% of each run, Pallas kernels for 0% -> 0%
where the time goes in v1:
time: 285 us; the launch traced here: 284 us
  blocking collectives  148 us (52%)
  waiting for transfers between devices  48.4 us (17%)
  matrix products  32 us (11%)
  starting transfers between devices  21 us (7%)
  between operations  13.6 us (5%)
  local copies, waits for them, and re-layouts  12.3 us (4%)
  other arithmetic  8.58 us (3%)
    all_to_all x2, blocking collectives, handle(): lax.all_to_all(jnp.stack([received] * lax.axis_size('tp')), 'tp', 0, 0)  104 us
    all_to_all x2, blocking collectives, exchange_in_groups(): lax.all_to_all(group, axis, split_axis=split_dim, concat_axis=concat_dim,...  44.5 us
    reduce_scatter x2, waiting for transfers between devices, run_expert(): lax.psum_scatter(down_term.astype(jnp.bfloat16), 'tp', scatter_dimension=...  34.5 us
    dot_general x2, matrix products, run_expert(): jnp.einsum('rf,fc->rc', hidden, w_down[0], preferred_element_type=jnp.flo...  24.2 us
    all_to_all x2, starting transfers between devices, run_expert(): return lax.all_to_all(shares, 'ep', split_axis=0, concat_axis=0, tiled=True)  15.1 us
    all_to_all x2, waiting for transfers between devices, run_expert(): return lax.all_to_all(shares, 'ep', split_axis=0, concat_axis=0, tiled=True)  13.8 us
    all_to_all x1, starting transfers between devices, from_everyone(): lax.all_to_all(jnp.broadcast_to(value[None], (length, *value.shape)), axi...  5.84 us
  transfers between devices with their start and end apart: 5, of which 2 were waited for; matrix products, arithmetic and copies ran while one was open for 9% of the time, Pallas kernels for 0%

profile of v1, /device:TPU:1, one launch (start us, length us, event | category | flops | bytes accessed | tf_op | source)
XLA Modules:
  0.0 284.4 jit_solution(3998032185391487300)
XLA Ops:
  6.5 1.4 fusion.11
  8.0 0.6 broadcast_in_dim.21
  8.6 5.8 %all-to-all-start = ((f32[4,1,256]{2,1,0:T(1,128)}), f32[4,1,256]{2,1,0:T(1,128)S(1)}, u32[]{:S(2)}, u32[]{:S(2)}) async-start(f32[4,1,256]{2,1,0:T(1,128)} %broadcast_in_dim.21), calls=%async_computation | async-start | bytes 8192 | tf_op jit(solution)/shard_map/all_to_all | solution.py:14
  14.4 0.7 convert_reduce_fusion
  15.2 0.6 reduce-window.6
  15.8 0.2 slice_reduce_fusion
  16.0 0.1 fusion.46
  16.1 0.8 select_reduce_fusion.1
  16.8 0.7 add_select_fusion
  17.5 0.1 copy.33
  17.7 1.7 fusion.10
  19.4 0.7 convert_element_type.41
  20.1 0.0 all-to-all-done
  20.1 2.0 convolution_convert_fusion.2
  22.1 0.1 fusion.49
  22.2 23.5 %all_to_all.36 = bf16[32,8,1792]{2,1,0:T(8,128)(2,1)S(1)} all-to-all(bf16[32,8,1792]{2,1,0:T(8,128)(2,1)S(1)} %get-tuple-element.5), channel_id=1, replica_groups=mesh['ep'=32,'tp'=4] {'ep'}, dimensions={0} | all-to-all | bytes 1835008 | tf_op jit(solution)/shard_map/all_to_all | solution.py:37
  45.7 0.2 stack.4
  46.0 0.0 slice-start
  46.0 46.9 %all_to_all.37 = bf16[4,32,8,1792]{3,2,1,0:T(8,128)(2,1)S(1)} all-to-all(bf16[4,32,8,1792]{3,2,1,0:T(8,128)(2,1)S(1)} %stack.4), channel_id=1, replica_groups=mesh['ep'=32,'tp'=4] {'tp'}, dimensions={0} | all-to-all | bytes 7340032 | tf_op jit(solution)/shard_map/all_to_all | solution.py:88
  92.8 2.8 copy.48
  95.7 0.7 copy.41
  96.3 0.0 copy-start
  96.4 1.8 copy-done
  98.2 0.0 slice-done.1
  98.2 2.1 fusion.8
  100.3 12.1 %convolution_convert_fusion.1 = bf16[256,7168]{1,0:T(8,128)(2,1)} fusion(bf16[1,512,7168]{2,1,0:T(8,128)(2,1)} %param.13, bf16[256,7168]{1,0:T(8,128)(2,1)} %bitcast.72, bf16[1,7168,512]{2,1,0:T(8,128)(2,1)} %param.12, f32[256,512]{1,0:T(8,128)S(1)} %fusion.8), kind=kOutput, calls=%fused_computation.1 | convolution fusion | flops 3760717824 | bytes 22544384 | tf_op jit(solution)/shard_map/rf,fc->rc/dot_general | solution.py:67
  112.4 0.0 reduce-scatter.3.cloned.1.call-update
  112.4 0.0 reduce-scatter.5.cloned.1.call-start
  112.5 21.0 %all_to_all.38 = bf16[32,8,1792]{2,1,0:T(8,128)(2,1)S(1)} all-to-all(bf16[32,8,1792]{2,1,0:T(8,128)(2,1)S(1)} %get-tuple-element.6), channel_id=1, replica_groups=mesh['ep'=32,'tp'=4] {'ep'}, dimensions={0} | all-to-all | bytes 1835008 | tf_op jit(solution)/shard_map/all_to_all | solution.py:37
  133.5 0.2 stack.5
  133.7 0.0 slice-start.2
  133.7 57.1 %all_to_all.39 = bf16[4,32,8,1792]{3,2,1,0:T(8,128)(2,1)S(1)} all-to-all(bf16[4,32,8,1792]{3,2,1,0:T(8,128)(2,1)S(1)} %stack.5), channel_id=1, replica_groups=mesh['ep'=32,'tp'=4] {'tp'}, dimensions={0} | all-to-all | bytes 7340032 | tf_op jit(solution)/shard_map/all_to_all | solution.py:88
  190.9 2.8 copy.47
  193.7 0.7 copy.42
  194.4 1.9 copy-done.1
  196.3 2.1 fusion.6
  198.4 12.1 %convolution_convert_fusion = bf16[256,7168]{1,0:T(8,128)(2,1)} fusion(bf16[1,512,7168]{2,1,0:T(8,128)(2,1)} %param.13, bf16[256,7168]{1,0:T(8,128)(2,1)} %bitcast.74, bf16[1,7168,512]{2,1,0:T(8,128)(2,1)} %param.12, f32[256,512]{1,0:T(8,128)S(1)} %fusion.6), kind=kOutput, calls=%fused_computation | convolution fusion | flops 3760717824 | bytes 22544384 | tf_op jit(solution)/shard_map/rf,fc->rc/dot_general | solution.py:67
  210.5 0.0 reduce-scatter.5.cloned.1.call-update
  210.6 0.0 reduce-scatter.3.cloned.1.call-done
  210.6 7.5 %all-to-all-start.3 = ((bf16[32,8,1792]{2,1,0:T(8,128)(2,1)}), bf16[32,8,1792]{2,1,0:T(8,128)(2,1)S(1)}, u32[]{:S(2)}, u32[]{:S(2)}) async-start(bf16[32,8,1792]{2,1,0:T(8,128)(2,1)} %bitcast.75), calls=%async_computation.4 | async-start | bytes 1835008 | tf_op jit(solution)/shard_map/all_to_all | solution.py:70
  218.1 34.5 %reduce-scatter.5.cloned.1.call-done = bf16[256,1792]{1,0:T(8,128)(2,1)} async-done(((bf16[256,7168]{1,0:T(8,128)(2,1)}), bf16[256,1792]{1,0:T(8,128)(2,1)}) %reduce-scatter.5.cloned.1.call-update) | async-done | bytes 917520 | tf_op jit(solution)/shard_map/reduce_scatter | solution.py:68
  252.6 0.0 all-to-all-done.3
  252.6 7.6 %all-to-all-start.6 = ((bf16[32,8,1792]{2,1,0:T(8,128)(2,1)}), bf16[32,8,1792]{2,1,0:T(8,128)(2,1)S(1)}, u32[]{:S(2)}, u32[]{:S(2)}) async-start(bf16[32,8,1792]{2,1,0:T(8,128)(2,1)} %bitcast.76), calls=%async_computation.8 | async-start | bytes 1835008 | tf_op jit(solution)/shard_map/all_to_all | solution.py:70
  260.2 0.1 copy.34
  260.3 1.7 select_reduce_fusion
  262.0 13.8 %all-to-all-done.6 = bf16[32,8,1792]{2,1,0:T(8,128)(2,1)S(1)} async-done(((bf16[32,8,1792]{2,1,0:T(8,128)(2,1)}), bf16[32,8,1792]{2,1,0:T(8,128)(2,1)S(1)}, u32[]{:S(2)}, u32[]{:S(2)}) %all-to-all-start.6) | async-done | bytes 917536 | tf_op jit(solution)/shard_map/all_to_all | solution.py:70
  275.9 0.1 pad_maximum_fusion
  276.0 1.6 convolution_convert_fusion.3
  (16 shorter events, 0.1 us)
Async XLA Ops:
  8.6 11.5 %all-to-all-start = ((f32[4,1,256]{2,1,0:T(1,128)}), f32[4,1,256]{2,1,0:T(1,128)S(1)}, u32[]{:S(2)}, u32[]{:S(2)}) async-start(f32[4,1,256]{2,1,0:T(1,128)} %broadcast_in_dim.21), calls=%async_computation | async-start | bytes 8192 | tf_op jit(solution)/shard_map/all_to_all | solution.py:14
  14.4 196.2 %reduce-scatter.3.cloned.1.call-start = ((), (), s32[]{:S(2)}) async-start(), calls=%async_computation.9 | async-start | bytes 4587520 | tf_op jit(solution)/shard_map/reduce_scatter | solution.py:68
  46.0 52.2 %slice-start = ((s8[7340032]{0:T(1024)(128)(4,1)}), s8[4194304]{0:T(1024)(128)(4,1)S(1)}, s32[]{:S(2)}) async-start(s8[7340032]{0:T(1024)(128)(4,1)} %bitcast.77), calls=%async_computation.11 | async-start | bytes 8388608
  92.8 5.3 %slice-start.1 = ((s8[7340032]{0:T(1024)(128)(4,1)}), s8[3145728]{0:T(1024)(128)(4,1)S(1)}, s32[]{:S(2)}) async-start(s8[7340032]{0:T(1024)(128)(4,1)} %bitcast.77), calls=%async_computation.12 | async-start | bytes 6291456
  96.3 1.8 copy-start
  112.4 140.2 %reduce-scatter.5.cloned.1.call-start = ((), (), s32[]{:S(2)}) async-start(), calls=%async_computation.10 | async-start | bytes 4587520 | tf_op jit(solution)/shard_map/reduce_scatter | solution.py:68
  133.7 62.5 %slice-start.2 = ((s8[7340032]{0:T(1024)(128)(4,1)}), s8[4194304]{0:T(1024)(128)(4,1)S(1)}, s32[]{:S(2)}) async-start(s8[7340032]{0:T(1024)(128)(4,1)} %bitcast.79), calls=%async_computation.13 | async-start | bytes 8388608
  190.9 5.4 %slice-start.3 = ((s8[7340032]{0:T(1024)(128)(4,1)}), s8[3145728]{0:T(1024)(128)(4,1)S(1)}, s32[]{:S(2)}) async-start(s8[7340032]{0:T(1024)(128)(4,1)} %bitcast.79), calls=%async_computation.14 | async-start | bytes 6291456
  194.4 1.9 copy-start.1
  210.5 49.7 %copy-start.2 = (bf16[256,8]{0,1:T(8,128)(2,1)S(1)}, bf16[256,8]{0,1:T(8,128)(2,1)}, u32[]{:S(2)}) copy-start(bf16[256,8]{0,1:T(8,128)(2,1)} %param.10) | copy-start | bytes 12292
  210.6 42.0 %all-to-all-start.3 = ((bf16[32,8,1792]{2,1,0:T(8,128)(2,1)}), bf16[32,8,1792]{2,1,0:T(8,128)(2,1)S(1)}, u32[]{:S(2)}, u32[]{:S(2)}) async-start(bf16[32,8,1792]{2,1,0:T(8,128)(2,1)} %bitcast.75), calls=%async_computation.4 | async-start | bytes 1835008 | tf_op jit(solution)/shard_map/all_to_all | solution.py:70
  252.6 23.3 %all-to-all-start.6 = ((bf16[32,8,1792]{2,1,0:T(8,128)(2,1)}), bf16[32,8,1792]{2,1,0:T(8,128)(2,1)S(1)}, u32[]{:S(2)}, u32[]{:S(2)}) async-start(bf16[32,8,1792]{2,1,0:T(8,128)(2,1)} %bitcast.76), calls=%async_computation.8 | async-start | bytes 1835008 | tf_op jit(solution)/shard_map/all_to_all | solution.py:70
Sparse Core Ops, SparseCore 0:
  112.5 59.4 reduce-scatter.2
  210.7 41.8 reduce-scatter.4
